TPU v7x, 8 devices: a whole 2x2x1 slice. The times are simulated.
8 devices in a mesh: dp: 1 (over z), ep: 8 (over x, y, core).
Axes of the slice: x: 2, y: 2, z: 1, core: 2. Of those that a mesh axis runs over, the one named last changes fastest.
Arguments:
- x: bfloat16 [1, 8, 256, 3584], P('dp', 'ep')
- expert: int32 [1, 8, 256, 2], P('dp', 'ep')
- slot: int32 [1, 8, 256, 2], P('dp', 'ep')
- gate: float32 [1, 8, 256, 2], P('dp', 'ep')
- w_gate: bfloat16 [16, 3584, 4864], P('ep')
- w_up: bfloat16 [16, 3584, 4864], P('ep')
- w_down: bfloat16 [16, 4864, 3584], P('ep')
Outputs:
- y: bfloat16 [1, 8, 256, 3584], P('dp', 'ep')
All inputs are finite; a program needn't handle non-finite values.
Results may differ from a plain program's by a relative error of at most 0.009.
Values are sent between devices in bfloat16 or wider.
A program may use at most 2 GiB of HBM per device.

v0:
```python
import jax
import jax.numpy as jnp
from jax import lax
from jax.sharding import NamedSharding, PartitionSpec as P


def einsum(form, a, b):
    return jnp.einsum(form, a.astype(jnp.float32), b.astype(jnp.float32))


def solution(mesh):
    def placed(v, *spec):
        return lax.with_sharding_constraint(v, NamedSharding(mesh, P(*spec)))

    def step(x, expert, slot, gate, w_gate, w_up, w_down):
        experts, (tokens, top) = w_gate.shape[0], expert.shape[2:]
        slots = 5 * tokens * top // (4 * experts)
        to_expert = jax.nn.one_hot(expert, experts, dtype=jnp.bfloat16)
        to_slot = jax.nn.one_hot(slot, slots, dtype=jnp.bfloat16)
        weighted = to_expert * gate[..., None].astype(jnp.bfloat16)
        dispatch = einsum("abtke,abtkc->abtec", to_expert, to_slot).astype(jnp.bfloat16)
        combine = einsum("abtke,abtkc->abtec", weighted, to_slot).astype(jnp.bfloat16)
        z = einsum("abtec,abtd->aebcd", dispatch, x).astype(jnp.bfloat16)
        z = placed(z, "dp", None, "ep", None, None)
        z = placed(z, "dp", "ep", None, None, None)
        h = jax.nn.silu(einsum("aebcd,edf->aebcf", z, w_gate))
        h = (h * einsum("aebcd,edf->aebcf", z, w_up)).astype(jnp.bfloat16)
        out = einsum("aebcf,efd->aebcd", h, w_down).astype(jnp.bfloat16)
        out = placed(out, "dp", "ep", None, None, None)
        out = placed(out, "dp", None, "ep", None, None)
        y = einsum("abtec,aebcd->abtd", combine, out)
        return y.astype(jnp.bfloat16)

    return step
```

profile of v0, /device:TPU:0, one launch (start us, length us, event | category | flops | bytes accessed | tf_op | source)
XLA Modules:
  0.0 235.2 jit_solution(17561108727197282621)
XLA Ops:
  0.0 0.0 copy-start
  0.0 0.9 copy.11
  1.0 0.8 copy.9
  1.8 2.0 convolution_convert_fusion.1
  3.8 0.0 copy-done
  3.8 1.5 convolution_convert_fusion
  5.3 57.0 %all-to-all.4 = bf16[1,8,2,1,40,3584]{5,4,2,3,0,1:T(8,128)(2,1)} all-to-all(bf16[1,8,2,1,40,3584]{5,4,2,3,0,1:T(8,128)(2,1)S(1)} %bitcast.115), channel_id=1, replica_groups=mesh['dp'=1,'ep'=8] {'ep'}, dimensions={1} | all-to-all | bytes 9175040 | tf_op jit(solution)/sharding_constraint;jit(solution)/sharding_constraint | solution.py:13
  62.4 35.8 %fusion.4 = f32[2,8,40,4864]{3,2,1,0:T(8,128)} fusion(bf16[2,3584,4864]{2,1,0:T(8,128)(2,1)} %param.4, bf16[1,8,2,1,40,3584]{5,4,2,3,0,1:T(8,128)(2,1)} %all-to-all.4), kind=kOutput, calls=%fused_computation.4 | convolution fusion | flops 22313697280 | bytes 86769664 | tf_op jit(solution)/aebcd,edf->aebcf/dot_general | solution.py:8
  98.2 35.8 %fusion.12 = bf16[2,8,40,4864]{3,2,1,0:T(8,128)(2,1)} fusion(bf16[2,3584,4864]{2,1,0:T(8,128)(2,1)} %param.5, f32[2,8,40,4864]{3,2,1,0:T(8,128)} %fusion.4, bf16[1,8,2,1,40,3584]{5,4,2,3,0,1:T(8,128)(2,1)} %all-to-all.4), kind=kOutput, calls=%fused_computation.13 | convolution fusion | flops 22332375040 | bytes 92995584 | tf_op jit(solution)/aebcd,edf->aebcf/dot_general | solution.py:8
  134.0 35.5 %fusion.18 = bf16[1,2,8,1,40,3584]{5,4,2,1,3,0:T(8,128)(2,1)} fusion(bf16[2,8,40,4864]{3,2,1,0:T(8,128)(2,1)} %fusion.12, bf16[2,4864,3584]{2,1,0:T(8,128)(2,1)} %param.6), kind=kOutput, calls=%fused_computation.16 | convolution fusion | flops 22315991040 | bytes 80543744 | tf_op jit(solution)/aebcf,efd->aebcd/dot_general | solution.py:8
  169.4 4.9 %copy.15 = bf16[1,2,8,1,40,3584]{5,4,1,3,0,2:T(8,128)(2,1)} copy(bf16[1,2,8,1,40,3584]{5,4,2,1,3,0:T(8,128)(2,1)} %fusion.18) | data formatting | bytes 9175040 | tf_op jit(solution)/sharding_constraint;jit(solution)/sharding_constraint | solution.py:13
  174.3 0.0 copy-start.1
  174.3 3.4 %all-to-all-start.1 = ((bf16[1,2,8,1,40,3584]{5,4,1,3,0,2:T(8,128)(2,1)}), bf16[1,2,8,1,40,3584]{5,4,1,3,0,2:T(8,128)(2,1)}, u32[]{:S(2)}, u32[]{:S(2)}) async-start(bf16[1,2,8,1,40,3584]{5,4,1,3,0,2:T(8,128)(2,1)} %copy.15), calls=%async_computation.1 | async-start | bytes 9175040 | tf_op jit(solution)/sharding_constraint;jit(solution)/sharding_constraint | solution.py:13
  177.8 0.0 copy-done.1
  177.8 0.1 copy.10
  177.9 2.4 %convolution_convert_fusion.2 = bf16[256,16,40]{2,1,0:T(8,128)(2,1)S(1)} fusion(s32[256,2]{1,0:T(8,128)S(1)} %copy.11, s32[256,2]{1,0:T(8,128)S(1)} %copy.9, bf16[256,2]{1,0:T(8,128)(2,1)S(1)} %copy.10), kind=kOutput, calls=%fused_computation.26 | convolution fusion | flops 856064 | bytes 332800 | tf_op jit(solution)/abtke,abtkc->abtec/dot_general | solution.py:8
  180.4 49.5 %all-to-all-done.1 = bf16[1,2,8,1,40,3584]{5,4,1,3,0,2:T(8,128)(2,1)} async-done(((bf16[1,2,8,1,40,3584]{5,4,1,3,0,2:T(8,128)(2,1)}), bf16[1,2,8,1,40,3584]{5,4,1,3,0,2:T(8,128)(2,1)}, u32[]{:S(2)}, u32[]{:S(2)}) %all-to-all-start.1) | async-done | bytes 4587552 | tf_op jit(solution)/sharding_constraint;jit(solution)/sharding_constraint | solution.py:13
  229.8 5.3 %fusion.22 = bf16[1,1,256,3584]{3,2,1,0:T(8,128)(2,1)} fusion(bf16[16,40,3584]{2,1,0:T(8,128)(2,1)} %bitcast.38, bf16[256,16,40]{2,1,0:T(8,128)(2,1)S(1)} %convolution_convert_fusion.2), kind=kOutput, calls=%fused_computation.19 | convolution fusion | flops 1175322624 | bytes 6750208 | tf_op jit(solution)/abtec,aebcd->abtd/dot_general | solution.py:8
  (1 shorter events, 0.0 us)
Async XLA Ops:
  0.0 3.8 %copy-start = (bf16[1,1,256,3584]{3,2,1,0:T(8,128)(2,1)S(1)}, bf16[1,1,256,3584]{3,2,1,0:T(8,128)(2,1)}, u32[]{:S(2)}) copy-start(bf16[1,1,256,3584]{3,2,1,0:T(8,128)(2,1)} %param.3) | copy-start | bytes 5505028
  174.3 3.5 %copy-start.1 = (f32[1,1,256,2]{2,3,1,0:T(2,128)S(1)}, f32[1,1,256,2]{2,3,1,0:T(2,128)}, u32[]{:S(2)}) copy-start(f32[1,1,256,2]{2,3,1,0:T(2,128)} %param.1) | copy-start | bytes 6148
  174.3 55.5 %all-to-all-start.1 = ((bf16[1,2,8,1,40,3584]{5,4,1,3,0,2:T(8,128)(2,1)}), bf16[1,2,8,1,40,3584]{5,4,1,3,0,2:T(8,128)(2,1)}, u32[]{:S(2)}, u32[]{:S(2)}) async-start(bf16[1,2,8,1,40,3584]{5,4,1,3,0,2:T(8,128)(2,1)} %copy.15), calls=%async_computation.1 | async-start | bytes 9175040 | tf_op jit(solution)/sharding_constraint;jit(solution)/sharding_constraint | solution.py:13
where the time goes:
time: 235 us
  matrix products  118 us (50%)
  blocking collectives  57 us (24%)
  waiting for transfers between devices  49.5 us (21%)
  local copies, waits for them, and re-layouts  6.78 us (3%)
  starting transfers between devices  3.45 us (1%)
    dot_general x7, matrix products, einsum(): return jnp.einsum(form, a.astype(jnp.float32), b.astype(jnp.float32))  118 us
    another operation x1, blocking collectives, placed(): return lax.with_sharding_constraint(v, NamedSharding(mesh, P(*spec)))  57 us
    another operation x1, waiting for transfers between devices, placed(): return lax.with_sharding_constraint(v, NamedSharding(mesh, P(*spec)))  49.5 us
    another operation x1, local copies, waits for them, and re-layouts, placed(): return lax.with_sharding_constraint(v, NamedSharding(mesh, P(*spec)))  4.87 us
  transfers between devices with their start and end apart: 1, of which 1 were waited for; matrix products, arithmetic and copies ran while one was open for 1% of the time, Pallas kernels for 0%

commit v1 on v0

v1 whole, which is shorter than its diff:
```python
import functools

import jax
import jax.numpy as jnp
from jax import lax
from jax.experimental import pallas as pl
from jax.experimental.pallas import tpu as pltpu
from jax.sharding import PartitionSpec as P

MESH = pl.DeviceIdType.MESH
BF = jnp.bfloat16
F32 = jnp.float32


def peer(me, r):
    x, y, c = me // 4, (me // 2) % 2, me % 2
    return ((x + r // 4) % 2) * 4 + ((y + (r // 2) % 2) % 2) * 2 + (c + r % 2) % 2


def block_of(o, r):
    a, b = slice(32 * r, 32 * r + 32), slice(256 + 8 * r, 264 + 8 * r)
    return jnp.concatenate([o[a, :256], o[b, :256], o[b, 256:], o[a, 256:]], axis=0).astype(BF)


def kernel(dims, x_ref, ex_ref, sl_ref, gt_ref, wg_ref, wu_ref, wd_ref, y_ref,
           x_buf, to_slots, weigh, send, z_in, back, z, acc, h, w_in, w_out,
           x_sem, in_sem, out_sem, send_sem, z_sem, back_send_sem, back_sem, y_sem):
    d, ff, chunks, slots, depth_in, depth_out = dims
    tokens = 256
    me = lax.axis_index("ep")

    def w_in_copy(e, k, m, slot):
        src = (wg_ref, wu_ref)[m]
        return pltpu.make_async_copy(src.at[e, pl.ds(k * 512, 512), :], w_in.at[slot], in_sem.at[slot])

    def w_out_copy(e, c, slot):
        return pltpu.make_async_copy(wd_ref.at[e, :, pl.ds(pl.multiple_of(c * 512, 512), 512)], w_out.at[slot],
                                     out_sem.at[slot])

    def x_copy(k):
        return pltpu.make_async_copy(x_ref.at[:, pl.ds(pl.multiple_of(k * 512, 512), 512)], x_buf.at[k], x_sem.at[k])

    barrier = pltpu.get_barrier_semaphore()
    for r in range(1, 8):
        pl.semaphore_signal(barrier, inc=1, device_id={"ep": peer(me, r)}, device_id_type=MESH)

    for k in range(chunks):
        x_copy(k).start()
    for i in range(depth_in):
        w_in_copy(0, i // 2, i % 2, i).start()
    for i in range(depth_out):
        w_out_copy(0, i, i).start()

    ex, sl = ex_ref[...], sl_ref[...]
    keep = sl < slots
    rel = jnp.bitwise_xor(ex // 2, me)
    half = ex % 2
    place = half * 320 + jnp.where(sl < 32, rel * 32 + sl, 256 + rel * 8 + sl - 32)
    place = jnp.where(keep, place, -1)
    p0, p1 = place[0:1, :], place[1:2, :]
    for e in range(2):
        row = lax.broadcasted_iota(jnp.int32, (320, tokens), 0) + 320 * e
        hit = jnp.where(row == p0, 1.0, jnp.where(row == p1, 1.0, 0.0))
        to_slots[e] = hit.astype(BF)

    pl.semaphore_wait(barrier, 7)

    def dispatch(i, _):
        e, k = i // chunks, i % chunks

        @pl.when(e == 0)
        def _():
            x_copy(k).wait()

        o = jnp.dot(to_slots[e], x_buf[k], preferred_element_type=F32)
        z_in[e, k, 0] = block_of(o, 0)
        for r in range(1, 8):
            send[e, k, r] = block_of(o, r)
        for r in (6, 2, 7, 3, 4, 5, 1):
            pltpu.make_async_remote_copy(
                src_ref=send.at[e, k, r], dst_ref=z_in.at[e, k, r], send_sem=send_sem.at[e], recv_sem=z_sem.at[e, k],
                device_id={"ep": peer(me, r)}, device_id_type=MESH).start()
        return 0

    lax.fori_loop(0, 2 * chunks, dispatch, 0)

    base = (half * 8 + rel) * 80
    left = jnp.where(keep, base + sl, -1).astype(F32)
    right = jnp.where(keep, base + jnp.where(sl < 32, 48 + sl, 8 + sl), -1).astype(F32)
    gt = gt_ref[...]
    rows = jnp.zeros((128, tokens), F32)
    line = lax.broadcasted_iota(jnp.int32, (128, tokens), 0)
    for i, v in enumerate((left[0:1], left[1:2], right[0:1], right[1:2], gt[0:1], gt[1:2])):
        rows = jnp.where(line == i, v, rows)
    down = rows.T
    col = lax.broadcasted_iota(jnp.int32, (tokens, 16 * 80), 1)
    for s in range(2):
        a0, a1 = (down[:, 2 * s + j:2 * s + j + 1].astype(jnp.int32) for j in range(2))
        weight = jnp.where(col == a0, down[:, 4:5], jnp.where(col == a1, down[:, 5:6], 0.0))
        weigh[s * tokens:(s + 1) * tokens, :] = weight.astype(BF)

    tiles = [(n, min(512, ff - n)) for n in range(0, ff, 512)]

    def clear(n, _):
        at = pl.ds(pl.multiple_of(n * 256, 256), 256)
        for m in range(2):
            acc[m, :, at] = jnp.zeros((320, 256), F32)
        return 0

    lax.fori_loop(0, ff // 256, clear, 0)

    def expert(e, _):
        def project(k, _):
            pltpu.make_async_copy(z_in.at[e, k, pl.ds(1, 7)], z_in.at[e, k, pl.ds(1, 7)], z_sem.at[e, k]).wait()
            for r in range(8):
                z[32 * r:32 * r + 32, 0:256] = z_in[e, k, r, 0:32, :]
                z[32 * r:32 * r + 32, 256:512] = z_in[e, k, r, 48:80, :]
            for r in range(0, 8, 2):
                a, b = z_in[e, k, r, 32:48, :].astype(F32), z_in[e, k, r + 1, 32:48, :].astype(F32)
                z[256 + 8 * r:272 + 8 * r, 0:256] = jnp.concatenate([a[:8], b[:8]], axis=0).astype(BF)
                z[256 + 8 * r:272 + 8 * r, 256:512] = jnp.concatenate([a[8:], b[8:]], axis=0).astype(BF)
            for m in range(2):
                i = (e * chunks + k) * 2 + m
                slot = i % depth_in
                w_in_copy(e, k, m, slot).wait()
                for n, w in tiles:
                    acc[m, :, n:n + w] += jnp.dot(z[...], w_in[slot, :, n:n + w], preferred_element_type=F32)
                later = i + depth_in
                for mm in range(2):
                    @pl.when(jnp.logical_and(later < 4 * chunks, later % 2 == mm))
                    def _():
                        w_in_copy(later // (2 * chunks), (later // 2) % chunks, mm, slot).start()
            return 0

        lax.fori_loop(0, chunks, project, 0)

        def activate(n, _):
            at = pl.ds(pl.multiple_of(n * 256, 256), 256)
            g, u = acc[0, :, at], acc[1, :, at]
            h[:, at] = (jax.nn.silu(g) * u).astype(BF)
            for m in range(2):
                acc[m, :, at] = jnp.zeros((320, 256), F32)
            return 0

        lax.fori_loop(0, ff // 256, activate, 0)

        pltpu.make_async_copy(send.at[e, :, pl.ds(1, 7)], send.at[e, :, pl.ds(1, 7)], send_sem.at[e]).wait()

        def finish(c, _):
            j = e * chunks + c
            slot = j % depth_out
            w_out_copy(e, c, slot).wait()
            o = jnp.dot(h[...], w_out[slot], preferred_element_type=F32)
            back[c, e, 0] = block_of(o, 0)
            for r in range(1, 8):
                send[e, c, r] = block_of(o, r)
            later = j + depth_out

            @pl.when(later < 2 * chunks)
            def _():
                w_out_copy(later // chunks, later % chunks, slot).start()

            for r in (6, 2, 7, 3, 4, 5, 1):
                pltpu.make_async_remote_copy(
                    src_ref=send.at[e, c, r], dst_ref=back.at[c, e, r], send_sem=back_send_sem.at[e],
                    recv_sem=back_sem.at[e, c], device_id={"ep": peer(me, r)}, device_id_type=MESH).start()
            return 0

        lax.fori_loop(0, chunks, finish, 0)
        return 0

    lax.fori_loop(0, 2, expert, 0)

    def y_copy(c, at):
        return pltpu.make_async_copy(x_buf.at[c], y_ref.at[:, pl.ds(pl.multiple_of(c * 512, 512), 512)], y_sem.at[at])

    def gather(c, _):
        for e in range(2):
            pltpu.make_async_copy(back.at[c, e, pl.ds(1, 7)], back.at[c, e, pl.ds(1, 7)], back_sem.at[e, c]).wait()
        o = jnp.dot(weigh[...], back[c].reshape(16 * 80, 256), preferred_element_type=F32)
        x_buf[c, :, 0:256] = o[:tokens].astype(BF)
        x_buf[c, :, 256:512] = o[tokens:].astype(BF)
        y_copy(c, c).start()
        return 0

    lax.fori_loop(0, chunks, gather, 0)
    for c in range(chunks):
        y_copy(c, c).wait()
    for e in range(2):
        pltpu.make_async_copy(send.at[e, :, pl.ds(1, 7)], send.at[e, :, pl.ds(1, 7)], back_send_sem.at[e]).wait()


def solution(mesh):
    def local(x, expert, slot, gate, w_gate, w_up, w_down):
        tokens, d = x.shape[2:]
        ff = w_gate.shape[2]
        top = expert.shape[3]
        chunks = d // 512
        slots = 5 * tokens * top // (4 * 8 * w_gate.shape[0])
        depth_in, depth_out = 3, 3
        anywhere = pl.BlockSpec(memory_space=pl.ANY)
        vmem = pl.BlockSpec(memory_space=pltpu.VMEM)
        y = pl.pallas_call(
            functools.partial(kernel, (d, ff, chunks, slots, depth_in, depth_out)),
            out_shape=jax.ShapeDtypeStruct((tokens, d), BF),
            in_specs=[anywhere, vmem, vmem, vmem, anywhere, anywhere, anywhere],
            out_specs=anywhere,
            scratch_shapes=[
                pltpu.VMEM((chunks, tokens, 512), BF),
                pltpu.VMEM((2, 320, tokens), BF),
                pltpu.VMEM((2 * tokens, 16 * 80), BF),
                pltpu.VMEM((2, chunks, 8, 80, 256), BF),
                pltpu.VMEM((2, chunks, 8, 80, 256), BF),
                pltpu.VMEM((chunks, 2, 8, 80, 256), BF),
                pltpu.VMEM((320, 512), BF),
                pltpu.VMEM((2, 320, ff), F32),
                pltpu.VMEM((320, ff), BF),
                pltpu.VMEM((depth_in, 512, ff), BF),
                pltpu.VMEM((depth_out, ff, 512), BF),
                pltpu.SemaphoreType.DMA((chunks,)),
                pltpu.SemaphoreType.DMA((depth_in,)),
                pltpu.SemaphoreType.DMA((depth_out,)),
                pltpu.SemaphoreType.DMA((2,)),
                pltpu.SemaphoreType.DMA((2, chunks)),
                pltpu.SemaphoreType.DMA((2,)),
                pltpu.SemaphoreType.DMA((2, chunks)),
                pltpu.SemaphoreType.DMA((chunks,)),
            ],
            compiler_params=pltpu.CompilerParams(collective_id=0, has_side_effects=True,
                                                 vmem_limit_bytes=67043328),
        )(x.reshape(tokens, d), expert.reshape(tokens, top).T, slot.reshape(tokens, top).T,
          gate.reshape(tokens, top).T,
          w_gate, w_up, w_down)
        return y.reshape(x.shape)

    tok = P("dp", "ep", None, None)
    wts = P("ep", None, None)
    return jax.shard_map(local, mesh=mesh, in_specs=(tok, tok, tok, tok, wts, wts, wts), out_specs=tok,
                         check_vma=False)
```

time: 235 us -> 116 us (0.49)
  matrix products: 118 us -> 0 us
  Pallas kernels: 0 us -> 113 us
  blocking collectives: 57 us -> 0 us
  waiting for transfers between devices: 49.5 us -> 0 us
  local copies, waits for them, and re-layouts: 6.78 us -> 2.85 us
  starting transfers between devices: 3.45 us -> 0 us
    dot_general x7 -> x0, matrix products: 118 us -> none  [einsum(): return jnp.einsum(form, a.astype(jnp.float32), b.astype(jnp.float32))]
    pallas_call x0 -> x1, Pallas kernels: none -> 113 us  [local(): pl.pallas_call(functools.partial(kernel, (d, ff, chunks, slots, depth_in,...]
    another operation x1 -> x0, blocking collectives: 57 us -> none  [placed(): return lax.with_sharding_constraint(v, NamedSharding(mesh, P(*spec)))]
    another operation x1 -> x0, waiting for transfers between devices: 49.5 us -> none  [placed(): return lax.with_sharding_constraint(v, NamedSharding(mesh, P(*spec)))]
    another operation x1 -> x0, local copies, waits for them, and re-layouts: 4.87 us -> none  [placed(): return lax.with_sharding_constraint(v, NamedSharding(mesh, P(*spec)))]
    another operation x1 -> x0, starting transfers between devices: 3.45 us -> none  [placed(): return lax.with_sharding_constraint(v, NamedSharding(mesh, P(*spec)))]
    unnamed x4 -> x1, local copies, waits for them, and re-layouts: 0.01 us -> 2.85 us
  transfers between devices with their start and end apart: 1 -> 0, of which waited for: 1 -> 0; matrix products, arithmetic and copies ran while one was open for 1% -> 0% of each run, Pallas kernels for 0% -> 0%
where the time goes in v1:
time: 116 us
  Pallas kernels  113 us (97%)
  local copies, waits for them, and re-layouts  2.85 us (2%)
    pallas_call x1, Pallas kernels, local(): pl.pallas_call(functools.partial(kernel, (d, ff, chunks, slots, depth_in,...  113 us
    unnamed x1, local copies, waits for them, and re-layouts  2.85 us

profile of v1, /device:TPU:0, one launch (start us, length us, event | category | flops | bytes accessed | tf_op | source)
XLA Modules:
  0.0 116.0 jit_solution(12886388305830337900)
XLA Ops:
  0.0 113.2 %shard_map.73 = bf16[256,3584]{1,0:T(8,128)(2,1)} custom-call(bf16[256,3584]{1,0:T(8,128)(2,1)} %bitcast.12, s32[2,256]{1,0:T(2,128)} %bitcast.13, s32[2,256]{1,0:T(2,128)} %bitcast.14, f32[2,256]{1,0:T(2,128)} %bitcast.15, bf16[2,3584,4864]{2,1,0:T(8,128)(2,1)} %wg_ref.1, bf16[2,3584,4864]{2,1,0:T(8,128)(2,1)} %wu_ref.1, bf16[2,4864,3584]{2,1,0:T(8,128)(2,1)} %wd_ref.1), custom_call_target="tpu_custom_call" | custom-call | tf_op jit(solution)/shard_map/pallas_call | solution.py:203
  113.2 2.8 %copy.9 = bf16[1,1,256,3584]{3,2,1,0:T(8,128)(2,1)} copy(bf16[1,1,256,3584]{3,2,1,0:T(8,128)(2,1)} %bitcast.11) | data formatting | bytes 3670016

commit v2 on v1

--- a/solution.py
+++ b/solution.py
@@ -46,10 +46,6 @@
 
     for k in range(chunks):
         x_copy(k).start()
-    for i in range(depth_in):
-        w_in_copy(0, i // 2, i % 2, i).start()
-    for i in range(depth_out):
-        w_out_copy(0, i, i).start()
 
     ex, sl = ex_ref[...], sl_ref[...]
     keep = sl < slots
@@ -63,15 +59,14 @@
         hit = jnp.where(row == p0, 1.0, jnp.where(row == p1, 1.0, 0.0))
         to_slots[e] = hit.astype(BF)
 
+    for k in range(chunks):
+        x_copy(k).wait()
+    for i in range(depth_in):
+        w_in_copy(0, i // 2, i % 2, i).start()
     pl.semaphore_wait(barrier, 7)
 
     def dispatch(i, _):
         e, k = i // chunks, i % chunks
-
-        @pl.when(e == 0)
-        def _():
-            x_copy(k).wait()
-
         o = jnp.dot(to_slots[e], x_buf[k], preferred_element_type=F32)
         z_in[e, k, 0] = block_of(o, 0)
         for r in range(1, 8):
@@ -84,30 +79,10 @@
 
     lax.fori_loop(0, 2 * chunks, dispatch, 0)
 
-    base = (half * 8 + rel) * 80
-    left = jnp.where(keep, base + sl, -1).astype(F32)
-    right = jnp.where(keep, base + jnp.where(sl < 32, 48 + sl, 8 + sl), -1).astype(F32)
-    gt = gt_ref[...]
-    rows = jnp.zeros((128, tokens), F32)
-    line = lax.broadcasted_iota(jnp.int32, (128, tokens), 0)
-    for i, v in enumerate((left[0:1], left[1:2], right[0:1], right[1:2], gt[0:1], gt[1:2])):
-        rows = jnp.where(line == i, v, rows)
-    down = rows.T
-    col = lax.broadcasted_iota(jnp.int32, (tokens, 16 * 80), 1)
-    for s in range(2):
-        a0, a1 = (down[:, 2 * s + j:2 * s + j + 1].astype(jnp.int32) for j in range(2))
-        weight = jnp.where(col == a0, down[:, 4:5], jnp.where(col == a1, down[:, 5:6], 0.0))
-        weigh[s * tokens:(s + 1) * tokens, :] = weight.astype(BF)
+    for i in range(depth_out):
+        w_out_copy(0, i, i).start()
 
     tiles = [(n, min(512, ff - n)) for n in range(0, ff, 512)]
-
-    def clear(n, _):
-        at = pl.ds(pl.multiple_of(n * 256, 256), 256)
-        for m in range(2):
-            acc[m, :, at] = jnp.zeros((320, 256), F32)
-        return 0
-
-    lax.fori_loop(0, ff // 256, clear, 0)
 
     def expert(e, _):
         def project(k, _):
@@ -124,7 +99,8 @@
                 slot = i % depth_in
                 w_in_copy(e, k, m, slot).wait()
                 for n, w in tiles:
-                    acc[m, :, n:n + w] += jnp.dot(z[...], w_in[slot, :, n:n + w], preferred_element_type=F32)
+                    part = jnp.dot(z[...], w_in[slot, :, n:n + w], preferred_element_type=F32)
+                    acc[m, :, n:n + w] = jnp.where(k == 0, 0.0, acc[m, :, n:n + w]) + part
                 later = i + depth_in
                 for mm in range(2):
                     @pl.when(jnp.logical_and(later < 4 * chunks, later % 2 == mm))
@@ -138,8 +114,6 @@
             at = pl.ds(pl.multiple_of(n * 256, 256), 256)
             g, u = acc[0, :, at], acc[1, :, at]
             h[:, at] = (jax.nn.silu(g) * u).astype(BF)
-            for m in range(2):
-                acc[m, :, at] = jnp.zeros((320, 256), F32)
             return 0
 
         lax.fori_loop(0, ff // 256, activate, 0)
@@ -170,6 +144,21 @@
         return 0
 
     lax.fori_loop(0, 2, expert, 0)
+
+    base = (half * 8 + rel) * 80
+    left = jnp.where(keep, base + sl, -1).astype(F32)
+    right = jnp.where(keep, base + jnp.where(sl < 32, 48 + sl, 8 + sl), -1).astype(F32)
+    gt = gt_ref[...]
+    rows = jnp.zeros((128, tokens), F32)
+    line = lax.broadcasted_iota(jnp.int32, (128, tokens), 0)
+    for i, v in enumerate((left[0:1], left[1:2], right[0:1], right[1:2], gt[0:1], gt[1:2])):
+        rows = jnp.where(line == i, v, rows)
+    down = rows.T
+    col = lax.broadcasted_iota(jnp.int32, (tokens, 16 * 80), 1)
+    for s in range(2):
+        a0, a1 = (down[:, 2 * s + j:2 * s + j + 1].astype(jnp.int32) for j in range(2))
+        weight = jnp.where(col == a0, down[:, 4:5], jnp.where(col == a1, down[:, 5:6], 0.0))
+        weigh[s * tokens:(s + 1) * tokens, :] = weight.astype(BF)
 
     def y_copy(c, at):
         return pltpu.make_async_copy(x_buf.at[c], y_ref.at[:, pl.ds(pl.multiple_of(c * 512, 512), 512)], y_sem.at[at])

time: 116 us -> 112 us (0.966)
  Pallas kernels: 113 us -> 109 us
    pallas_call x1, Pallas kernels: 113 us -> 109 us  [local(): pl.pallas_call(functools.partial(kernel, (d, ff, chunks, slots, depth_in,...]
where the time goes in v2:
time: 112 us
  Pallas kernels  109 us (97%)
  local copies, waits for them, and re-layouts  2.85 us (3%)
    pallas_call x1, Pallas kernels, local(): pl.pallas_call(functools.partial(kernel, (d, ff, chunks, slots, depth_in,...  109 us
    unnamed x1, local copies, waits for them, and re-layouts  2.85 us

profile of v2, /device:TPU:0, one launch (start us, length us, event | category | flops | bytes accessed | tf_op | source)
XLA Modules:
  0.0 112.0 jit_solution(2789488624421021880)
XLA Ops:
  0.0 109.2 %shard_map.73 = bf16[256,3584]{1,0:T(8,128)(2,1)} custom-call(bf16[256,3584]{1,0:T(8,128)(2,1)} %bitcast.12, s32[2,256]{1,0:T(2,128)} %bitcast.13, s32[2,256]{1,0:T(2,128)} %bitcast.14, f32[2,256]{1,0:T(2,128)} %bitcast.15, bf16[2,3584,4864]{2,1,0:T(8,128)(2,1)} %wg_ref.1, bf16[2,3584,4864]{2,1,0:T(8,128)(2,1)} %wu_ref.1, bf16[2,4864,3584]{2,1,0:T(8,128)(2,1)} %wd_ref.1), custom_call_target="tpu_custom_call" | custom-call | tf_op jit(solution)/shard_map/pallas_call | solution.py:192
  109.2 2.8 %copy.9 = bf16[1,1,256,3584]{3,2,1,0:T(8,128)(2,1)} copy(bf16[1,1,256,3584]{3,2,1,0:T(8,128)(2,1)} %bitcast.11) | data formatting | bytes 3670016

commit v3 on v2

--- a/solution.py
+++ b/solution.py
@@ -82,10 +82,11 @@
     for i in range(depth_out):
         w_out_copy(0, i, i).start()
 
-    tiles = [(n, min(512, ff - n)) for n in range(0, ff, 512)]
+    tiles = [(slice(0, 320), n, 512) for n in range(0, ff - 511, 512)]
+    tiles += [(slice(m, m + 160), ff - 256, 256) for m in (0, 160)]
 
     def expert(e, _):
-        def project(k, _):
+        def project(k, last):
             pltpu.make_async_copy(z_in.at[e, k, pl.ds(1, 7)], z_in.at[e, k, pl.ds(1, 7)], z_sem.at[e, k]).wait()
             for r in range(8):
                 z[32 * r:32 * r + 32, 0:256] = z_in[e, k, r, 0:32, :]
@@ -98,9 +99,16 @@
                 i = (e * chunks + k) * 2 + m
                 slot = i % depth_in
                 w_in_copy(e, k, m, slot).wait()
-                for n, w in tiles:
-                    part = jnp.dot(z[...], w_in[slot, :, n:n + w], preferred_element_type=F32)
-                    acc[m, :, n:n + w] = jnp.where(k == 0, 0.0, acc[m, :, n:n + w]) + part
+                for rows, n, w in tiles:
+                    at = slice(n, n + w)
+                    part = jnp.dot(z[rows, :], w_in[slot, :, at], preferred_element_type=F32)
+                    if not last:
+                        acc[m, rows, at] = jnp.where(k == 0, 0.0, acc[m, rows, at]) + part
+                    elif m == 0:
+                        acc[0, rows, at] += part
+                    else:
+                        g, u = acc[0, rows, at], acc[1, rows, at] + part
+                        h[rows, at] = (jax.nn.silu(g) * u).astype(BF)
                 later = i + depth_in
                 for mm in range(2):
                     @pl.when(jnp.logical_and(later < 4 * chunks, later % 2 == mm))
@@ -108,15 +116,8 @@
                         w_in_copy(later // (2 * chunks), (later // 2) % chunks, mm, slot).start()
             return 0
 
-        lax.fori_loop(0, chunks, project, 0)
-
-        def activate(n, _):
-            at = pl.ds(pl.multiple_of(n * 256, 256), 256)
-            g, u = acc[0, :, at], acc[1, :, at]
-            h[:, at] = (jax.nn.silu(g) * u).astype(BF)
-            return 0
-
-        lax.fori_loop(0, ff // 256, activate, 0)
+        lax.fori_loop(0, chunks - 1, lambda k, _: project(k, False), 0)
+        project(chunks - 1, True)
 
         pltpu.make_async_copy(send.at[e, :, pl.ds(1, 7)], send.at[e, :, pl.ds(1, 7)], send_sem.at[e]).wait()
 

time: 112 us -> 109 us (0.973)
  Pallas kernels: 109 us -> 106 us
    pallas_call x1, Pallas kernels: 109 us -> 106 us  [local(): pl.pallas_call(functools.partial(kernel, (d, ff, chunks, slots, depth_in,...]
where the time goes in v3:
time: 109 us
  Pallas kernels  106 us (97%)
  local copies, waits for them, and re-layouts  2.85 us (3%)
    pallas_call x1, Pallas kernels, local(): pl.pallas_call(functools.partial(kernel, (d, ff, chunks, slots, depth_in,...  106 us
    unnamed x1, local copies, waits for them, and re-layouts  2.85 us

profile of v3, /device:TPU:0, one launch (start us, length us, event | category | flops | bytes accessed | tf_op | source)
XLA Modules:
  0.0 109.2 jit_solution(7233963534239169179)
XLA Ops:
  0.0 106.4 %shard_map.73 = bf16[256,3584]{1,0:T(8,128)(2,1)} custom-call(bf16[256,3584]{1,0:T(8,128)(2,1)} %bitcast.12, s32[2,256]{1,0:T(2,128)} %bitcast.13, s32[2,256]{1,0:T(2,128)} %bitcast.14, f32[2,256]{1,0:T(2,128)} %bitcast.15, bf16[2,3584,4864]{2,1,0:T(8,128)(2,1)} %wg_ref.1, bf16[2,3584,4864]{2,1,0:T(8,128)(2,1)} %wu_ref.1, bf16[2,4864,3584]{2,1,0:T(8,128)(2,1)} %wd_ref.1), custom_call_target="tpu_custom_call" | custom-call | tf_op jit(solution)/shard_map/pallas_call | solution.py:193
  106.4 2.8 %copy.9 = bf16[1,1,256,3584]{3,2,1,0:T(8,128)(2,1)} copy(bf16[1,1,256,3584]{3,2,1,0:T(8,128)(2,1)} %bitcast.11) | data formatting | bytes 3670016

commit v4 on v3

--- a/solution.py
+++ b/solution.py
@@ -59,14 +59,15 @@
         hit = jnp.where(row == p0, 1.0, jnp.where(row == p1, 1.0, 0.0))
         to_slots[e] = hit.astype(BF)
 
-    for k in range(chunks):
-        x_copy(k).wait()
-    for i in range(depth_in):
-        w_in_copy(0, i // 2, i % 2, i).start()
     pl.semaphore_wait(barrier, 7)
 
     def dispatch(i, _):
         e, k = i // chunks, i % chunks
+
+        @pl.when(e == 0)
+        def _():
+            x_copy(k).wait()
+
         o = jnp.dot(to_slots[e], x_buf[k], preferred_element_type=F32)
         z_in[e, k, 0] = block_of(o, 0)
         for r in range(1, 8):
@@ -75,6 +76,12 @@
             pltpu.make_async_remote_copy(
                 src_ref=send.at[e, k, r], dst_ref=z_in.at[e, k, r], send_sem=send_sem.at[e], recv_sem=z_sem.at[e, k],
                 device_id={"ep": peer(me, r)}, device_id_type=MESH).start()
+
+        @pl.when(i == 2)
+        def _():
+            for j in range(depth_in):
+                w_in_copy(0, j // 2, j % 2, j).start()
+
         return 0
 
     lax.fori_loop(0, 2 * chunks, dispatch, 0)
@@ -178,6 +185,20 @@
         y_copy(c, c).wait()
     for e in range(2):
         pltpu.make_async_copy(send.at[e, :, pl.ds(1, 7)], send.at[e, :, pl.ds(1, 7)], back_send_sem.at[e]).wait()
+
+
+def settle(pieces, a_ref, o_ref, buf, in_sem, out_sem):
+    width = a_ref.shape[1] // pieces
+    at = [pl.ds(i * width, width) for i in range(pieces)]
+    reads = [pltpu.make_async_copy(a_ref.at[:, s], buf.at[i], in_sem.at[i]) for i, s in enumerate(at)]
+    writes = [pltpu.make_async_copy(buf.at[i], o_ref.at[:, s], out_sem.at[i]) for i, s in enumerate(at)]
+    for c in reads:
+        c.start()
+    for r, w in zip(reads, writes):
+        r.wait()
+        w.start()
+    for c in writes:
+        c.wait()
 
 
 def solution(mesh):
@@ -221,6 +242,15 @@
         )(x.reshape(tokens, d), expert.reshape(tokens, top).T, slot.reshape(tokens, top).T,
           gate.reshape(tokens, top).T,
           w_gate, w_up, w_down)
+        y = pl.pallas_call(
+            functools.partial(settle, chunks),
+            out_shape=jax.ShapeDtypeStruct((tokens, d), BF),
+            in_specs=[anywhere],
+            out_specs=anywhere,
+            scratch_shapes=[pltpu.VMEM((chunks, tokens, d // chunks), BF), pltpu.SemaphoreType.DMA((chunks,)),
+                            pltpu.SemaphoreType.DMA((chunks,))],
+            compiler_params=pltpu.CompilerParams(vmem_limit_bytes=60000000),
+        )(y)
         return y.reshape(x.shape)
 
     tok = P("dp", "ep", None, None)

time: 109 us -> 109 us (level)
  Pallas kernels: 106 us -> 109 us
  local copies, waits for them, and re-layouts: 2.85 us -> 0 us
    unnamed x1 -> x0, local copies, waits for them, and re-layouts: 2.85 us -> none
    pallas_call x0 -> x1, Pallas kernels: none -> 2.29 us  [local(): pl.pallas_call(functools.partial(settle, chunks), out_shape=jax.ShapeDtyp...]
where the time goes in v4:
time: 109 us
  Pallas kernels  109 us (100%)
    pallas_call x1, Pallas kernels, local(): pl.pallas_call(functools.partial(kernel, (d, ff, chunks, slots, depth_in,...  107 us
    pallas_call x1, Pallas kernels, local(): pl.pallas_call(functools.partial(settle, chunks), out_shape=jax.ShapeDtyp...  2.29 us

profile of v4, /device:TPU:0, one launch (start us, length us, event | category | flops | bytes accessed | tf_op | source)
XLA Modules:
  0.0 109.0 jit_solution(2562528198078801251)
XLA Ops:
  0.0 106.7 %shard_map.73.a_ref = bf16[256,3584]{1,0:T(8,128)(2,1)} custom-call(bf16[256,3584]{1,0:T(8,128)(2,1)} %bitcast.11, s32[2,256]{1,0:T(2,128)} %bitcast.12, s32[2,256]{1,0:T(2,128)} %bitcast.13, f32[2,256]{1,0:T(2,128)} %bitcast.14, bf16[2,3584,4864]{2,1,0:T(8,128)(2,1)} %wg_ref.1, bf16[2,3584,4864]{2,1,0:T(8,128)(2,1)} %wu_ref.1, bf16[2,4864,3584]{2,1,0:T(8,128)(2,1)} %wd_ref.1), custom_call_target="tpu_custom_call" | custom-call | tf_op jit(solution)/shard_map/pallas_call | solution.py:214
  106.7 2.3 %shard_map.74 = bf16[256,3584]{1,0:T(8,128)(2,1)} custom-call(bf16[256,3584]{1,0:T(8,128)(2,1)} %shard_map.73.a_ref), custom_call_target="tpu_custom_call" | custom-call | tf_op jit(solution)/shard_map/pallas_call | solution.py:245

commit v5 on v3

--- a/solution.py
+++ b/solution.py
@@ -23,8 +23,8 @@
 
 
 def kernel(dims, x_ref, ex_ref, sl_ref, gt_ref, wg_ref, wu_ref, wd_ref, y_ref,
-           x_buf, to_slots, weigh, send, z_in, back, z, acc, h, w_in, w_out,
-           x_sem, in_sem, out_sem, send_sem, z_sem, back_send_sem, back_sem, y_sem):
+           to_slots, weigh, send, z_in, back, z, acc, h, w_in, w_out,
+           x_sem, in_sem, out_sem, send_sem, z_sem, back_send_sem, back_sem):
     d, ff, chunks, slots, depth_in, depth_out = dims
     tokens = 256
     me = lax.axis_index("ep")
@@ -37,8 +37,11 @@
         return pltpu.make_async_copy(wd_ref.at[e, :, pl.ds(pl.multiple_of(c * 512, 512), 512)], w_out.at[slot],
                                      out_sem.at[slot])
 
+    def columns(k):
+        return pl.ds(pl.multiple_of(k * 512, 512), 512)
+
     def x_copy(k):
-        return pltpu.make_async_copy(x_ref.at[:, pl.ds(pl.multiple_of(k * 512, 512), 512)], x_buf.at[k], x_sem.at[k])
+        return pltpu.make_async_copy(x_ref.at[:, columns(k)], y_ref.at[:, columns(k)], x_sem.at[k])
 
     barrier = pltpu.get_barrier_semaphore()
     for r in range(1, 8):
@@ -59,15 +62,16 @@
         hit = jnp.where(row == p0, 1.0, jnp.where(row == p1, 1.0, 0.0))
         to_slots[e] = hit.astype(BF)
 
-    for k in range(chunks):
-        x_copy(k).wait()
-    for i in range(depth_in):
-        w_in_copy(0, i // 2, i % 2, i).start()
     pl.semaphore_wait(barrier, 7)
 
     def dispatch(i, _):
         e, k = i // chunks, i % chunks
-        o = jnp.dot(to_slots[e], x_buf[k], preferred_element_type=F32)
+
+        @pl.when(e == 0)
+        def _():
+            x_copy(k).wait()
+
+        o = jnp.dot(to_slots[e], y_ref[:, columns(k)], preferred_element_type=F32)
         z_in[e, k, 0] = block_of(o, 0)
         for r in range(1, 8):
             send[e, k, r] = block_of(o, r)
@@ -75,6 +79,12 @@
             pltpu.make_async_remote_copy(
                 src_ref=send.at[e, k, r], dst_ref=z_in.at[e, k, r], send_sem=send_sem.at[e], recv_sem=z_sem.at[e, k],
                 device_id={"ep": peer(me, r)}, device_id_type=MESH).start()
+
+        @pl.when(i == 2)
+        def _():
+            for j in range(depth_in):
+                w_in_copy(0, j // 2, j % 2, j).start()
+
         return 0
 
     lax.fori_loop(0, 2 * chunks, dispatch, 0)
@@ -161,21 +171,15 @@
         weight = jnp.where(col == a0, down[:, 4:5], jnp.where(col == a1, down[:, 5:6], 0.0))
         weigh[s * tokens:(s + 1) * tokens, :] = weight.astype(BF)
 
-    def y_copy(c, at):
-        return pltpu.make_async_copy(x_buf.at[c], y_ref.at[:, pl.ds(pl.multiple_of(c * 512, 512), 512)], y_sem.at[at])
-
     def gather(c, _):
         for e in range(2):
             pltpu.make_async_copy(back.at[c, e, pl.ds(1, 7)], back.at[c, e, pl.ds(1, 7)], back_sem.at[e, c]).wait()
         o = jnp.dot(weigh[...], back[c].reshape(16 * 80, 256), preferred_element_type=F32)
-        x_buf[c, :, 0:256] = o[:tokens].astype(BF)
-        x_buf[c, :, 256:512] = o[tokens:].astype(BF)
-        y_copy(c, c).start()
+        y_ref[:, pl.ds(pl.multiple_of(c * 512, 512), 256)] = o[:tokens].astype(BF)
+        y_ref[:, pl.ds(pl.multiple_of(c * 512 + 256, 256), 256)] = o[tokens:].astype(BF)
         return 0
 
     lax.fori_loop(0, chunks, gather, 0)
-    for c in range(chunks):
-        y_copy(c, c).wait()
     for e in range(2):
         pltpu.make_async_copy(send.at[e, :, pl.ds(1, 7)], send.at[e, :, pl.ds(1, 7)], back_send_sem.at[e]).wait()
 
@@ -192,11 +196,10 @@
         vmem = pl.BlockSpec(memory_space=pltpu.VMEM)
         y = pl.pallas_call(
             functools.partial(kernel, (d, ff, chunks, slots, depth_in, depth_out)),
-            out_shape=jax.ShapeDtypeStruct((tokens, d), BF),
+            out_shape=pltpu.VMEM((tokens, d), BF),
             in_specs=[anywhere, vmem, vmem, vmem, anywhere, anywhere, anywhere],
-            out_specs=anywhere,
+            out_specs=vmem,
             scratch_shapes=[
-                pltpu.VMEM((chunks, tokens, 512), BF),
                 pltpu.VMEM((2, 320, tokens), BF),
                 pltpu.VMEM((2 * tokens, 16 * 80), BF),
                 pltpu.VMEM((2, chunks, 8, 80, 256), BF),
@@ -214,10 +217,9 @@
                 pltpu.SemaphoreType.DMA((2, chunks)),
                 pltpu.SemaphoreType.DMA((2,)),
                 pltpu.SemaphoreType.DMA((2, chunks)),
-                pltpu.SemaphoreType.DMA((chunks,)),
             ],
             compiler_params=pltpu.CompilerParams(collective_id=0, has_side_effects=True,
-                                                 vmem_limit_bytes=67043328),
+                                                 vmem_limit_bytes=64500000),
         )(x.reshape(tokens, d), expert.reshape(tokens, top).T, slot.reshape(tokens, top).T,
           gate.reshape(tokens, top).T,
           w_gate, w_up, w_down)

time: 109 us -> 107 us (0.982)
  local copies, waits for them, and re-layouts: 2.85 us -> 1.23 us
    unnamed x1, local copies, waits for them, and re-layouts: 2.85 us -> 1.23 us
where the time goes in v5:
time: 107 us
  Pallas kernels  106 us (99%)
  local copies, waits for them, and re-layouts  1.23 us (1%)
    pallas_call x1, Pallas kernels, local(): pl.pallas_call(functools.partial(kernel, (d, ff, chunks, slots, depth_in,...  106 us

profile of v5, /device:TPU:0, one launch (start us, length us, event | category | flops | bytes accessed | tf_op | source)
XLA Modules:
  0.0 107.1 jit_solution(12526793069851288483)
XLA Ops:
  0.0 105.9 %shard_map.73 = bf16[256,3584]{1,0:T(8,128)(2,1)S(1)} custom-call(bf16[256,3584]{1,0:T(8,128)(2,1)} %bitcast.12, s32[2,256]{1,0:T(2,128)} %bitcast.13, s32[2,256]{1,0:T(2,128)} %bitcast.14, f32[2,256]{1,0:T(2,128)} %bitcast.15, bf16[2,3584,4864]{2,1,0:T(8,128)(2,1)} %wg_ref.1, bf16[2,3584,4864]{2,1,0:T(8,128)(2,1)} %wu_ref.1, bf16[2,4864,3584]{2,1,0:T(8,128)(2,1)} %wd_ref.1), custom_call_target="tpu_custom_call" | custom-call | tf_op jit(solution)/shard_map/pallas_call | solution.py:197
  105.9 1.2 %copy.9 = bf16[1,1,256,3584]{3,2,1,0:T(8,128)(2,1)} copy(bf16[1,1,256,3584]{3,2,1,0:T(8,128)(2,1)S(1)} %bitcast.11) | data formatting | bytes 3670016

commit v6 on v5

--- a/solution.py
+++ b/solution.py
@@ -40,15 +40,16 @@
     def columns(k):
         return pl.ds(pl.multiple_of(k * 512, 512), 512)
 
-    def x_copy(k):
-        return pltpu.make_async_copy(x_ref.at[:, columns(k)], y_ref.at[:, columns(k)], x_sem.at[k])
+    def x_copy(part):
+        at = (pl.ds(0, 512), pl.ds(512, d - 512))[part]
+        return pltpu.make_async_copy(x_ref.at[:, at], y_ref.at[:, at], x_sem.at[part])
 
     barrier = pltpu.get_barrier_semaphore()
     for r in range(1, 8):
         pl.semaphore_signal(barrier, inc=1, device_id={"ep": peer(me, r)}, device_id_type=MESH)
 
-    for k in range(chunks):
-        x_copy(k).start()
+    for part in range(2):
+        x_copy(part).start()
 
     ex, sl = ex_ref[...], sl_ref[...]
     keep = sl < slots
@@ -57,37 +58,40 @@
     place = half * 320 + jnp.where(sl < 32, rel * 32 + sl, 256 + rel * 8 + sl - 32)
     place = jnp.where(keep, place, -1)
     p0, p1 = place[0:1, :], place[1:2, :]
-    for e in range(2):
+    def choose(e):
         row = lax.broadcasted_iota(jnp.int32, (320, tokens), 0) + 320 * e
         hit = jnp.where(row == p0, 1.0, jnp.where(row == p1, 1.0, 0.0))
         to_slots[e] = hit.astype(BF)
 
-    pl.semaphore_wait(barrier, 7)
-
-    def dispatch(i, _):
-        e, k = i // chunks, i % chunks
-
-        @pl.when(e == 0)
-        def _():
-            x_copy(k).wait()
-
+    def collect(e, k):
         o = jnp.dot(to_slots[e], y_ref[:, columns(k)], preferred_element_type=F32)
         z_in[e, k, 0] = block_of(o, 0)
         for r in range(1, 8):
             send[e, k, r] = block_of(o, r)
+
+    def post(e, k):
         for r in (6, 2, 7, 3, 4, 5, 1):
             pltpu.make_async_remote_copy(
                 src_ref=send.at[e, k, r], dst_ref=z_in.at[e, k, r], send_sem=send_sem.at[e], recv_sem=z_sem.at[e, k],
                 device_id={"ep": peer(me, r)}, device_id_type=MESH).start()
 
-        @pl.when(i == 2)
-        def _():
-            for j in range(depth_in):
-                w_in_copy(0, j // 2, j % 2, j).start()
-
-        return 0
-
-    lax.fori_loop(0, 2 * chunks, dispatch, 0)
+    choose(0)
+    x_copy(0).wait()
+    collect(0, 0)
+    pl.semaphore_wait(barrier, 7)
+    post(0, 0)
+    x_copy(1).wait()
+    for i in range(depth_in):
+        w_in_copy(0, i // 2, i % 2, i).start()
+
+    def dispatch(i, _):
+        collect(i // chunks, i % chunks)
+        post(i // chunks, i % chunks)
+        return 0
+
+    lax.fori_loop(1, chunks, dispatch, 0)
+    choose(1)
+    lax.fori_loop(chunks, 2 * chunks, dispatch, 0)
 
     for i in range(depth_out):
         w_out_copy(0, i, i).start()
@@ -148,7 +152,7 @@
             for r in (6, 2, 7, 3, 4, 5, 1):
                 pltpu.make_async_remote_copy(
                     src_ref=send.at[e, c, r], dst_ref=back.at[c, e, r], send_sem=back_send_sem.at[e],
-                    recv_sem=back_sem.at[e, c], device_id={"ep": peer(me, r)}, device_id_type=MESH).start()
+                    recv_sem=back_sem.at[e * (1 + c)], device_id={"ep": peer(me, r)}, device_id_type=MESH).start()
             return 0
 
         lax.fori_loop(0, chunks, finish, 0)
@@ -171,14 +175,27 @@
         weight = jnp.where(col == a0, down[:, 4:5], jnp.where(col == a1, down[:, 5:6], 0.0))
         weigh[s * tokens:(s + 1) * tokens, :] = weight.astype(BF)
 
+    pltpu.make_async_copy(back.at[:, 0, pl.ds(1, 7)], back.at[:, 0, pl.ds(1, 7)], back_sem.at[0]).wait()
+
+    def share(c, e):
+        o = jnp.dot(weigh[:, 640 * e:640 * (e + 1)], back[c, e].reshape(640, 256), preferred_element_type=F32)
+        return o[:tokens], o[tokens:]
+
+    def first(c, _):
+        o = share(c, 0)
+        for m in range(2):
+            acc[m, 0:tokens, pl.ds(pl.multiple_of(c * 256, 256), 256)] = o[m]
+        return 0
+
     def gather(c, _):
-        for e in range(2):
-            pltpu.make_async_copy(back.at[c, e, pl.ds(1, 7)], back.at[c, e, pl.ds(1, 7)], back_sem.at[e, c]).wait()
-        o = jnp.dot(weigh[...], back[c].reshape(16 * 80, 256), preferred_element_type=F32)
-        y_ref[:, pl.ds(pl.multiple_of(c * 512, 512), 256)] = o[:tokens].astype(BF)
-        y_ref[:, pl.ds(pl.multiple_of(c * 512 + 256, 256), 256)] = o[tokens:].astype(BF)
-        return 0
-
+        pltpu.make_async_copy(back.at[c, 1, pl.ds(1, 7)], back.at[c, 1, pl.ds(1, 7)], back_sem.at[1 + c]).wait()
+        o = share(c, 1)
+        for m in range(2):
+            y = acc[m, 0:tokens, pl.ds(pl.multiple_of(c * 256, 256), 256)] + o[m]
+            y_ref[:, pl.ds(pl.multiple_of(c * 512 + 256 * m, 256), 256)] = y.astype(BF)
+        return 0
+
+    lax.fori_loop(0, chunks, first, 0)
     lax.fori_loop(0, chunks, gather, 0)
     for e in range(2):
         pltpu.make_async_copy(send.at[e, :, pl.ds(1, 7)], send.at[e, :, pl.ds(1, 7)], back_send_sem.at[e]).wait()
@@ -210,13 +227,13 @@
                 pltpu.VMEM((320, ff), BF),
                 pltpu.VMEM((depth_in, 512, ff), BF),
                 pltpu.VMEM((depth_out, ff, 512), BF),
-                pltpu.SemaphoreType.DMA((chunks,)),
+                pltpu.SemaphoreType.DMA((2,)),
                 pltpu.SemaphoreType.DMA((depth_in,)),
                 pltpu.SemaphoreType.DMA((depth_out,)),
                 pltpu.SemaphoreType.DMA((2,)),
                 pltpu.SemaphoreType.DMA((2, chunks)),
                 pltpu.SemaphoreType.DMA((2,)),
-                pltpu.SemaphoreType.DMA((2, chunks)),
+                pltpu.SemaphoreType.DMA((1 + chunks,)),
             ],
             compiler_params=pltpu.CompilerParams(collective_id=0, has_side_effects=True,
                                                  vmem_limit_bytes=64500000),

time: 107 us -> 107 us (level)
  no operation moved by 1% of the time
where the time goes in v6:
time: 107 us; the launch traced here: 106 us
  Pallas kernels  105 us (98%)
  local copies, waits for them, and re-layouts  1.23 us (1%)
    pallas_call x1, Pallas kernels, local(): pl.pallas_call(functools.partial(kernel, (d, ff, chunks, slots, depth_in,...  105 us

profile of v6, /device:TPU:0, one launch (start us, length us, event | category | flops | bytes accessed | tf_op | source)
XLA Modules:
  0.0 106.4 jit_solution(12510811014084333285)
XLA Ops:
  0.0 105.2 %shard_map.73 = bf16[256,3584]{1,0:T(8,128)(2,1)S(1)} custom-call(bf16[256,3584]{1,0:T(8,128)(2,1)} %bitcast.12, s32[2,256]{1,0:T(2,128)} %bitcast.13, s32[2,256]{1,0:T(2,128)} %bitcast.14, f32[2,256]{1,0:T(2,128)} %bitcast.15, bf16[2,3584,4864]{2,1,0:T(8,128)(2,1)} %wg_ref.1, bf16[2,3584,4864]{2,1,0:T(8,128)(2,1)} %wu_ref.1, bf16[2,4864,3584]{2,1,0:T(8,128)(2,1)} %wd_ref.1), custom_call_target="tpu_custom_call" | custom-call | tf_op jit(solution)/shard_map/pallas_call | solution.py:214
  105.2 1.2 %copy.9 = bf16[1,1,256,3584]{3,2,1,0:T(8,128)(2,1)} copy(bf16[1,1,256,3584]{3,2,1,0:T(8,128)(2,1)S(1)} %bitcast.11) | data formatting | bytes 3670016

commit v7 on v6

--- a/solution.py
+++ b/solution.py
@@ -22,9 +22,9 @@
     return jnp.concatenate([o[a, :256], o[b, :256], o[b, 256:], o[a, 256:]], axis=0).astype(BF)
 
 
-def kernel(dims, x_ref, ex_ref, sl_ref, gt_ref, wg_ref, wu_ref, wd_ref, y_ref,
-           to_slots, weigh, send, z_in, back, z, acc, h, w_in, w_out,
-           x_sem, in_sem, out_sem, send_sem, z_sem, back_send_sem, back_sem):
+def kernel(dims, x_ref, ex_hbm, sl_hbm, gt_hbm, wg_ref, wu_ref, wd_ref, y_ref,
+           ex_ref, sl_ref, gt_ref, to_slots, weigh, send, z_in, back, z, acc, h, w_in, w_out,
+           route_sem, x_sem, in_sem, out_sem, send_sem, z_sem, back_send_sem, back_sem):
     d, ff, chunks, slots, depth_in, depth_out = dims
     tokens = 256
     me = lax.axis_index("ep")
@@ -48,8 +48,14 @@
     for r in range(1, 8):
         pl.semaphore_signal(barrier, inc=1, device_id={"ep": peer(me, r)}, device_id_type=MESH)
 
+    routes = [pltpu.make_async_copy(a, b, route_sem.at[i])
+              for i, (a, b) in enumerate(((ex_hbm, ex_ref), (sl_hbm, sl_ref), (gt_hbm, gt_ref)))]
+    for copy in routes:
+        copy.start()
     for part in range(2):
         x_copy(part).start()
+    for copy in routes:
+        copy.wait()
 
     ex, sl = ex_ref[...], sl_ref[...]
     keep = sl < slots
@@ -58,6 +64,7 @@
     place = half * 320 + jnp.where(sl < 32, rel * 32 + sl, 256 + rel * 8 + sl - 32)
     place = jnp.where(keep, place, -1)
     p0, p1 = place[0:1, :], place[1:2, :]
+
     def choose(e):
         row = lax.broadcasted_iota(jnp.int32, (320, tokens), 0) + 320 * e
         hit = jnp.where(row == p0, 1.0, jnp.where(row == p1, 1.0, 0.0))
@@ -214,9 +221,12 @@
         y = pl.pallas_call(
             functools.partial(kernel, (d, ff, chunks, slots, depth_in, depth_out)),
             out_shape=pltpu.VMEM((tokens, d), BF),
-            in_specs=[anywhere, vmem, vmem, vmem, anywhere, anywhere, anywhere],
+            in_specs=[anywhere] * 7,
             out_specs=vmem,
             scratch_shapes=[
+                pltpu.VMEM((top, tokens), jnp.int32),
+                pltpu.VMEM((top, tokens), jnp.int32),
+                pltpu.VMEM((top, tokens), F32),
                 pltpu.VMEM((2, 320, tokens), BF),
                 pltpu.VMEM((2 * tokens, 16 * 80), BF),
                 pltpu.VMEM((2, chunks, 8, 80, 256), BF),
@@ -227,6 +237,7 @@
                 pltpu.VMEM((320, ff), BF),
                 pltpu.VMEM((depth_in, 512, ff), BF),
                 pltpu.VMEM((depth_out, ff, 512), BF),
+                pltpu.SemaphoreType.DMA((3,)),
                 pltpu.SemaphoreType.DMA((2,)),
                 pltpu.SemaphoreType.DMA((depth_in,)),
                 pltpu.SemaphoreType.DMA((depth_out,)),

time: 107 us -> 107 us (level)
  no operation moved by 1% of the time
where the time goes in v7:
time: 107 us
  Pallas kernels  106 us (99%)
  local copies, waits for them, and re-layouts  1.23 us (1%)
    pallas_call x1, Pallas kernels, local(): pl.pallas_call(functools.partial(kernel, (d, ff, chunks, slots, depth_in,...  106 us

profile of v7, /device:TPU:0, one launch (start us, length us, event | category | flops | bytes accessed | tf_op | source)
XLA Modules:
  0.0 107.0 jit_solution(1876772073279271070)
XLA Ops:
  0.0 105.8 %shard_map.73 = bf16[256,3584]{1,0:T(8,128)(2,1)S(1)} custom-call(bf16[256,3584]{1,0:T(8,128)(2,1)} %bitcast.12, s32[2,256]{1,0:T(2,128)} %bitcast.13, s32[2,256]{1,0:T(2,128)} %bitcast.14, f32[2,256]{1,0:T(2,128)} %bitcast.15, bf16[2,3584,4864]{2,1,0:T(8,128)(2,1)} %wg_ref.1, bf16[2,3584,4864]{2,1,0:T(8,128)(2,1)} %wu_ref.1, bf16[2,4864,3584]{2,1,0:T(8,128)(2,1)} %wd_ref.1), custom_call_target="tpu_custom_call" | custom-call | tf_op jit(solution)/shard_map/pallas_call | solution.py:221
  105.8 1.2 %copy.9 = bf16[1,1,256,3584]{3,2,1,0:T(8,128)(2,1)} copy(bf16[1,1,256,3584]{3,2,1,0:T(8,128)(2,1)S(1)} %bitcast.11) | data formatting | bytes 3670016

commit v8 on v7

--- a/solution.py
+++ b/solution.py
@@ -43,6 +43,9 @@
     def x_copy(part):
         at = (pl.ds(0, 512), pl.ds(512, d - 512))[part]
         return pltpu.make_async_copy(x_ref.at[:, at], y_ref.at[:, at], x_sem.at[part])
+
+    turn = 2 * (me % 2)
+    order = (6 - turn, 2, 7 - turn, 3, 4 + turn, 5 + turn, 1)
 
     barrier = pltpu.get_barrier_semaphore()
     for r in range(1, 8):
@@ -77,7 +80,7 @@
             send[e, k, r] = block_of(o, r)
 
     def post(e, k):
-        for r in (6, 2, 7, 3, 4, 5, 1):
+        for r in order:
             pltpu.make_async_remote_copy(
                 src_ref=send.at[e, k, r], dst_ref=z_in.at[e, k, r], send_sem=send_sem.at[e], recv_sem=z_sem.at[e, k],
                 device_id={"ep": peer(me, r)}, device_id_type=MESH).start()
@@ -156,7 +159,7 @@
             def _():
                 w_out_copy(later // chunks, later % chunks, slot).start()
 
-            for r in (6, 2, 7, 3, 4, 5, 1):
+            for r in order:
                 pltpu.make_async_remote_copy(
                     src_ref=send.at[e, c, r], dst_ref=back.at[c, e, r], send_sem=back_send_sem.at[e],
                     recv_sem=back_sem.at[e * (1 + c)], device_id={"ep": peer(me, r)}, device_id_type=MESH).start()

time: 107 us -> 107 us (level)
  no operation moved by 1% of the time
where the time goes in v8:
time: 107 us
  Pallas kernels  106 us (99%)
  local copies, waits for them, and re-layouts  1.23 us (1%)
    pallas_call x1, Pallas kernels, local(): pl.pallas_call(functools.partial(kernel, (d, ff, chunks, slots, depth_in,...  106 us

profile of v8, /device:TPU:0, one launch (start us, length us, event | category | flops | bytes accessed | tf_op | source)
XLA Modules:
  0.0 107.0 jit_solution(5602620550737468362)
XLA Ops:
  0.0 105.8 %shard_map.73 = bf16[256,3584]{1,0:T(8,128)(2,1)S(1)} custom-call(bf16[256,3584]{1,0:T(8,128)(2,1)} %bitcast.12, s32[2,256]{1,0:T(2,128)} %bitcast.13, s32[2,256]{1,0:T(2,128)} %bitcast.14, f32[2,256]{1,0:T(2,128)} %bitcast.15, bf16[2,3584,4864]{2,1,0:T(8,128)(2,1)} %wg_ref.1, bf16[2,3584,4864]{2,1,0:T(8,128)(2,1)} %wu_ref.1, bf16[2,4864,3584]{2,1,0:T(8,128)(2,1)} %wd_ref.1), custom_call_target="tpu_custom_call" | custom-call | tf_op jit(solution)/shard_map/pallas_call | solution.py:224
  105.8 1.2 %copy.9 = bf16[1,1,256,3584]{3,2,1,0:T(8,128)(2,1)} copy(bf16[1,1,256,3584]{3,2,1,0:T(8,128)(2,1)S(1)} %bitcast.11) | data formatting | bytes 3670016

commit v9 on v7

--- a/solution.py
+++ b/solution.py
@@ -23,7 +23,7 @@
 
 
 def kernel(dims, x_ref, ex_hbm, sl_hbm, gt_hbm, wg_ref, wu_ref, wd_ref, y_ref,
-           ex_ref, sl_ref, gt_ref, to_slots, weigh, send, z_in, back, z, acc, h, w_in, w_out,
+           to_slots, weigh, send, z_in, back, z, acc, h, w_in, w_out, ex_ref, sl_ref, gt_ref,
            route_sem, x_sem, in_sem, out_sem, send_sem, z_sem, back_send_sem, back_sem):
     d, ff, chunks, slots, depth_in, depth_out = dims
     tokens = 256
@@ -224,9 +224,6 @@
             in_specs=[anywhere] * 7,
             out_specs=vmem,
             scratch_shapes=[
-                pltpu.VMEM((top, tokens), jnp.int32),
-                pltpu.VMEM((top, tokens), jnp.int32),
-                pltpu.VMEM((top, tokens), F32),
                 pltpu.VMEM((2, 320, tokens), BF),
                 pltpu.VMEM((2 * tokens, 16 * 80), BF),
                 pltpu.VMEM((2, chunks, 8, 80, 256), BF),
@@ -237,6 +234,9 @@
                 pltpu.VMEM((320, ff), BF),
                 pltpu.VMEM((depth_in, 512, ff), BF),
                 pltpu.VMEM((depth_out, ff, 512), BF),
+                pltpu.VMEM((top, tokens), jnp.int32),
+                pltpu.VMEM((top, tokens), jnp.int32),
+                pltpu.VMEM((top, tokens), F32),
                 pltpu.SemaphoreType.DMA((3,)),
                 pltpu.SemaphoreType.DMA((2,)),
                 pltpu.SemaphoreType.DMA((depth_in,)),

time: 107 us -> 106 us (level)
  Pallas kernels: 106 us -> 104 us
    pallas_call x1, Pallas kernels: 106 us -> 104 us  [local(): pl.pallas_call(functools.partial(kernel, (d, ff, chunks, slots, depth_in,...]
where the time goes in v9:
time: 106 us
  Pallas kernels  104 us (98%)
  local copies, waits for them, and re-layouts  1.23 us (1%)
    pallas_call x1, Pallas kernels, local(): pl.pallas_call(functools.partial(kernel, (d, ff, chunks, slots, depth_in,...  104 us

profile of v9, /device:TPU:0, one launch (start us, length us, event | category | flops | bytes accessed | tf_op | source)
XLA Modules:
  0.0 105.7 jit_solution(4799983150461182425)
XLA Ops:
  0.0 104.5 %shard_map.73 = bf16[256,3584]{1,0:T(8,128)(2,1)S(1)} custom-call(bf16[256,3584]{1,0:T(8,128)(2,1)} %bitcast.12, s32[2,256]{1,0:T(2,128)} %bitcast.13, s32[2,256]{1,0:T(2,128)} %bitcast.14, f32[2,256]{1,0:T(2,128)} %bitcast.15, bf16[2,3584,4864]{2,1,0:T(8,128)(2,1)} %wg_ref.1, bf16[2,3584,4864]{2,1,0:T(8,128)(2,1)} %wu_ref.1, bf16[2,4864,3584]{2,1,0:T(8,128)(2,1)} %wd_ref.1), custom_call_target="tpu_custom_call" | custom-call | tf_op jit(solution)/shard_map/pallas_call | solution.py:221
  104.5 1.2 %copy.9 = bf16[1,1,256,3584]{3,2,1,0:T(8,128)(2,1)} copy(bf16[1,1,256,3584]{3,2,1,0:T(8,128)(2,1)S(1)} %bitcast.11) | data formatting | bytes 3670016

commit v10 on v9

--- a/solution.py
+++ b/solution.py
@@ -23,7 +23,7 @@
 
 
 def kernel(dims, x_ref, ex_hbm, sl_hbm, gt_hbm, wg_ref, wu_ref, wd_ref, y_ref,
-           to_slots, weigh, send, z_in, back, z, acc, h, w_in, w_out, ex_ref, sl_ref, gt_ref,
+           send, z_in, back, z, acc, h, w_in, w_out, to_slots, weigh, ex_ref, sl_ref, gt_ref,
            route_sem, x_sem, in_sem, out_sem, send_sem, z_sem, back_send_sem, back_sem):
     d, ff, chunks, slots, depth_in, depth_out = dims
     tokens = 256
@@ -224,8 +224,6 @@
             in_specs=[anywhere] * 7,
             out_specs=vmem,
             scratch_shapes=[
-                pltpu.VMEM((2, 320, tokens), BF),
-                pltpu.VMEM((2 * tokens, 16 * 80), BF),
                 pltpu.VMEM((2, chunks, 8, 80, 256), BF),
                 pltpu.VMEM((2, chunks, 8, 80, 256), BF),
                 pltpu.VMEM((chunks, 2, 8, 80, 256), BF),
@@ -234,6 +232,8 @@
                 pltpu.VMEM((320, ff), BF),
                 pltpu.VMEM((depth_in, 512, ff), BF),
                 pltpu.VMEM((depth_out, ff, 512), BF),
+                pltpu.VMEM((2, 320, tokens), BF),
+                pltpu.VMEM((2 * tokens, 16 * 80), BF),
                 pltpu.VMEM((top, tokens), jnp.int32),
                 pltpu.VMEM((top, tokens), jnp.int32),
                 pltpu.VMEM((top, tokens), F32),

time: 106 us -> 106 us (level)
  no operation moved by 1% of the time
where the time goes in v10:
time: 106 us
  Pallas kernels  104 us (98%)
  local copies, waits for them, and re-layouts  1.23 us (1%)
    pallas_call x1, Pallas kernels, local(): pl.pallas_call(functools.partial(kernel, (d, ff, chunks, slots, depth_in,...  104 us

profile of v10, /device:TPU:0, one launch (start us, length us, event | category | flops | bytes accessed | tf_op | source)
XLA Modules:
  0.0 105.7 jit_solution(14312284806902751287)
XLA Ops:
  0.0 104.5 %shard_map.73 = bf16[256,3584]{1,0:T(8,128)(2,1)S(1)} custom-call(bf16[256,3584]{1,0:T(8,128)(2,1)} %bitcast.12, s32[2,256]{1,0:T(2,128)} %bitcast.13, s32[2,256]{1,0:T(2,128)} %bitcast.14, f32[2,256]{1,0:T(2,128)} %bitcast.15, bf16[2,3584,4864]{2,1,0:T(8,128)(2,1)} %wg_ref.1, bf16[2,3584,4864]{2,1,0:T(8,128)(2,1)} %wu_ref.1, bf16[2,4864,3584]{2,1,0:T(8,128)(2,1)} %wd_ref.1), custom_call_target="tpu_custom_call" | custom-call | tf_op jit(solution)/shard_map/pallas_call | solution.py:221
  104.5 1.2 %copy.9 = bf16[1,1,256,3584]{3,2,1,0:T(8,128)(2,1)} copy(bf16[1,1,256,3584]{3,2,1,0:T(8,128)(2,1)S(1)} %bitcast.11) | data formatting | bytes 3670016
